TPU v7x, 128 devices: a whole 4x4x4 slice. The times are simulated.
128 devices in a mesh: mem: 16 (over y, x), pix: 8 (over z, core).
Axes of the slice: x: 4, y: 4, z: 4, core: 2. Of those that a mesh axis runs over, the one named last changes fastest.
Arguments:
- prior_motion: bfloat16 [64, 16, 262144], P('mem', None, 'pix'), may hold values from -6 to 6
- measured_motion: float32 [1200], replicated, may hold values from -1.6 to 1.6
- measurement_noise_stddev: float32 [1200], replicated, may hold values from 0.05 to 0.5
- gaussian_jitter: float32 [2, 1200, 64], replicated, may hold values from -6 to 6
- scene_couples: int32 [2, 1200], replicated, may hold values from 0 to 15, as said below
- targeted_tile_number: int32 [1200], replicated, may hold values from 0 to 4095
Outputs:
- analysis: bfloat16 [64, 16, 262144], P('mem', None, 'pix')
Inputs may be any that keep to these rules, and one draw needn't show every extreme that they name: scene_couples[0, k] < scene_couples[1, k]: row 0 holds the earlier acquisition, row 1 the later.
All inputs are finite; a program needn't handle non-finite values.
Results may differ from a plain program's by a relative error of at most 0.011.
Values may be sent and summed in bfloat16 or wider, within the bound.
A program may use at most 128 MiB of HBM per device.

v0:
```python
import math

import jax
import jax.numpy as jnp
from jax import lax
from jax.sharding import PartitionSpec as P

BLK = 64
PASS_COUNT = 2


def block_sums(pieces):
    part_cells = pieces.shape[2]
    block_count = part_cells // BLK
    summer = (
        jnp.arange(part_cells, dtype=jnp.int32)[:, None] // BLK
        == jnp.arange(block_count, dtype=jnp.int32)[None, :]
    ).astype(jnp.bfloat16)
    flat = jnp.dot(pieces.reshape(-1, part_cells), summer, preferred_element_type=jnp.float32)
    return flat.reshape(pieces.shape[0], pieces.shape[1], block_count)


def with_sums(pieces):
    return (pieces, block_sums(pieces))


def to_pixels(ground_motion_vector):
    return with_sums(
        lax.all_to_all(ground_motion_vector, "mem", split_axis=2, concat_axis=0, tiled=True)
    )


def to_members(pixel_state):
    return lax.all_to_all(pixel_state, "mem", split_axis=0, concat_axis=2, tiled=True)


def predict(sums, picker):
    flat_sums = sums.reshape(sums.shape[0], -1)
    return (
        jnp.dot(
            picker, flat_sums.T, precision=lax.Precision.HIGHEST, preferred_element_type=jnp.float32
        )
        / BLK
    )


def member_terms(predicted, measured_motion, member_anomaly, noise):
    realization_vectors = predicted.shape[1]
    centred = predicted - jnp.mean(predicted, axis=1, keepdims=True)
    scaled = centred / (member_anomaly[:, None] * math.sqrt(realization_vectors - 1))
    misfit = (
        measured_motion[:, None] + member_anomaly[:, None] * noise - predicted
    ) / member_anomaly[:, None]
    return (scaled, misfit)


def products(scaled, misfit):
    gram = jnp.dot(
        scaled.T, scaled, precision=lax.Precision.HIGHEST, preferred_element_type=jnp.float32
    )
    cross = jnp.dot(
        scaled.T, misfit, precision=lax.Precision.HIGHEST, preferred_element_type=jnp.float32
    )
    return (gram, cross)


def solve_mixing(gram, cross):
    realization_vectors = gram.shape[0]
    factor = jnp.linalg.cholesky(jnp.eye(realization_vectors, dtype=jnp.float32) + gram)
    return (
        jax.scipy.linalg.cho_solve((factor, True), cross) / math.sqrt(realization_vectors - 1)
    ).astype(jnp.bfloat16)


def update(pixel_state, mixing):
    realization_vectors = pixel_state.shape[0]
    average = jnp.sum(pixel_state, axis=0, dtype=jnp.float32) / realization_vectors
    anomaly = (pixel_state.astype(jnp.float32) - average).astype(jnp.bfloat16)
    change = jnp.dot(
        mixing.T, anomaly.reshape(realization_vectors, -1), preferred_element_type=jnp.float32
    )
    return (pixel_state.astype(jnp.float32) + change.reshape(pixel_state.shape)).astype(
        jnp.bfloat16
    )


def body(
    prior_motion,
    measured_motion,
    measurement_noise_stddev,
    gaussian_jitter,
    scene_couples,
    targeted_tile_number,
):
    cells_per_tile = prior_motion.shape[2]
    part_width = cells_per_tile // lax.axis_size("mem")
    local_blocks = part_width // BLK
    first_block = (
        lax.axis_index("pix") * cells_per_tile + lax.axis_index("mem") * part_width
    ) // BLK
    block_range = first_block + jnp.arange(local_blocks, dtype=jnp.int32)
    block_table = (targeted_tile_number[:, None] == block_range[None, :]).astype(jnp.float32)
    scene_timeline = jnp.arange(prior_motion.shape[1], dtype=jnp.int32)
    pair_table = (scene_timeline[None, :] == scene_couples[1][:, None]).astype(jnp.float32) - (
        scene_timeline[None, :] == scene_couples[0][:, None]
    ).astype(jnp.float32)
    picker = (pair_table[:, :, None] * block_table[:, None, :]).reshape(pair_table.shape[0], -1)
    member_anomaly = jnp.sqrt(jnp.float32(float(PASS_COUNT))) * measurement_noise_stddev
    pixel_state, sums = to_pixels(prior_motion)
    for iteration in range(PASS_COUNT):
        if iteration > 0:
            sums = block_sums(pixel_state)
        predicted = predict(sums, picker)
        scaled, misfit = member_terms(
            predicted, measured_motion, member_anomaly, gaussian_jitter[iteration]
        )
        gram, cross = lax.psum(products(scaled, misfit), ("mem", "pix"))
        pixel_state = update(pixel_state, solve_mixing(gram, cross))
    return to_members(pixel_state)


def solution(mesh):
    return jax.shard_map(
        body,
        mesh=mesh,
        in_specs=(P("mem", None, "pix"), P(), P(), P(), P(), P()),
        out_specs=P("mem", None, "pix"),
        check_vma=False,
    )
```

profile of v0, /device:TPU:1, one launch (start us, length us, event | category | flops | bytes accessed | tf_op | source)
XLA Modules:
  0.0 536.7 jit_solution(16468579744521945431)
XLA Ops:
  0.0 37.7 %copy.41 = bf16[4,16,32768]{1,0,2:T(4,128)(2,1)} copy(bf16[4,16,32768]{2,1,0:T(8,128)(2,1)} %param.9) | data formatting | bytes 8388608 | tf_op args[0]
  37.7 36.8 %reshape.195 = bf16[16,2,65536]{2,1,0:T(2,128)(2,1)} reshape(bf16[32768,4,16]{2,1,0:T(4,128)(2,1)} %bitcast.107) | data formatting | bytes 8388608
  74.6 0.0 copy-start.4
  74.6 7.8 %all-to-all-start = ((bf16[16,2,65536]{2,1,0:T(2,128)(2,1)}), bf16[16,2,65536]{2,1,0:T(2,128)(2,1)}, u32[]{:S(2)}, u32[]{:S(2)}) async-start(bf16[16,2,65536]{2,1,0:T(2,128)(2,1)} %reshape.195), calls=%async_computation | async-start | bytes 8388608 | tf_op jit(solution)/shard_map/all_to_all | solution.py:29
  82.4 0.0 copy-done.4
  82.5 0.0 copy-done.6
  82.5 0.1 compare_convert_fusion
  82.6 0.2 broadcast_multiply_fusion
  82.8 62.0 %all-to-all-done = bf16[16,2,65536]{2,1,0:T(2,128)(2,1)} async-done(((bf16[16,2,65536]{2,1,0:T(2,128)(2,1)}), bf16[16,2,65536]{2,1,0:T(2,128)(2,1)}, u32[]{:S(2)}, u32[]{:S(2)}) %all-to-all-start) | async-done | bytes 4194336 | tf_op jit(solution)/shard_map/all_to_all | solution.py:29
  144.8 25.6 %reshape.196 = bf16[32768,4,16]{2,1,0:T(4,128)(2,1)} reshape(bf16[16,2,65536]{2,1,0:T(2,128)(2,1)} %all-to-all-done) | data formatting | bytes 8388608
  170.4 44.3 %copy.66 = bf16[4,16,16,2048]{3,1,0,2:T(8,128)(2,1)} copy(bf16[4,16,16,2048]{1,0,3,2:T(4,128)(2,1)} %bitcast.105) | data formatting | bytes 8388608 | tf_op jit(solution)/shard_map/all_to_all | solution.py:29
  214.7 33.4 %copy.65 = bf16[4,16,16,2048]{3,2,1,0:T(8,128)(2,1)} copy(bf16[4,16,16,2048]{1,0,3,2:T(4,128)(2,1)} %bitcast.106) | data formatting | bytes 8388608 | tf_op jit(solution)/shard_map/all_to_all | solution.py:29
  248.1 0.0 copy-start.1
  248.1 3.4 bitcast_convert_fusion
  251.5 0.0 copy-done.1
  251.6 0.9 fusion.7
  252.5 2.3 copy-done
  254.8 8.1 %copy.48 = f32[16,4,16,2048]{3,2,1,0:T(8,128)} copy(f32[16,4,16,2048]{3,0,2,1:T(8,128)S(1)} %bitcast_convert_fusion) | data formatting | bytes 16777216 | tf_op jit(solution)/shard_map/convert_element_type | solution.py:82
  262.9 12.4 %copy.43 = f32[16,4,16,2048]{3,1,0,2:T(4,128)} copy(f32[16,4,16,2048]{3,0,2,1:T(8,128)} %copy-done) | data formatting | bytes 16777216 | tf_op jit(solution)/shard_map/convert_element_type | solution.py:82
  275.3 3.5 convolution_bitcast_fusion
  278.9 0.2 copy.45
  279.1 0.2 reshape_reshape.6
  279.3 0.0 copy-start.7
  279.3 1.8 fusion.56
  281.1 0.0 copy-done.5
  281.1 0.4 fusion.29
  281.6 0.0 copy-done.9
  281.6 0.0 copy-done.7
  281.6 0.5 fusion.25
  282.1 66.2 %all-reduce.1 = (f32[64,64]{1,0:T(8,128)S(1)}, f32[64,64]{0,1:T(8,128)S(1)}) all-reduce(f32[64,64]{1,0:T(8,128)S(1)} %fusion.25, f32[64,64]{0,1:T(8,128)S(1)} %fusion.29), channel_id=1, replica_groups=mesh['mem'=16,'pix'=8] {'mem','pix'}, use_global_device_ids=true, to_apply=%region_4.6 | all-reduce | flops 8192 | bytes 65536 | tf_op jit(solution)/shard_map/psum | solution.py:117
  348.2 0.1 copy.47
  348.3 5.8 %cholesky.44 = f32[64,64]{1,0:T(8,128)S(1)} custom-call(f32[64,64]{1,0:T(8,128)S(1)} %fusion.52), custom_call_target="Cholesky" | custom-call | tf_op jit(solution)/shard_map/jit(cholesky)/cholesky | solution.py:69
  354.2 0.6 compare_reduce_fusion.1
  354.8 0.7 fusion.43
  355.5 4.9 custom-call.8
  360.4 0.3 fusion.50
  360.7 0.2 fusion.11
  360.8 11.6 %copy.73 = f32[8,8,16,2048]{3,1,2,0:T(8,128)} copy(f32[8,8,16,2048]{3,2,1,0:T(8,128)} %bitcast.108) | data formatting | bytes 16777216
  372.5 10.4 %reshape.189 = f32[64,16,2048]{2,0,1:T(8,128)} reshape(f32[16,4,16,2048]{3,1,0,2:T(4,128)} %copy.43) | data formatting | bytes 16777216 | tf_op jit(solution)/shard_map/convert_element_type | solution.py:82
  382.9 0.0 copy-start.2
  382.9 4.1 subtract_convert_fusion
  387.0 1.7 copy-done.2
  388.7 1.4 convert_reduce_fusion
  390.1 0.0 copy-start.3
  390.1 2.3 copy.51
  392.4 0.0 copy-done.3
  392.4 1.4 fusion.12
  393.8 0.2 reshape_reshape.7
  394.0 1.8 fusion.57
  395.8 0.4 fusion.30
  396.3 0.0 copy-done.8
  396.3 0.5 fusion.20
  396.7 64.1 %all-reduce = (f32[64,64]{1,0:T(8,128)S(1)}, f32[64,64]{0,1:T(8,128)S(1)}) all-reduce(f32[64,64]{1,0:T(8,128)S(1)} %fusion.20, f32[64,64]{0,1:T(8,128)S(1)} %fusion.30), channel_id=1, replica_groups=mesh['mem'=16,'pix'=8] {'mem','pix'}, use_global_device_ids=true, to_apply=%region_8.11 | all-reduce | flops 8192 | bytes 65536 | tf_op jit(solution)/shard_map/psum | solution.py:117
  460.9 0.1 copy.54
  461.0 5.8 %cholesky.55 = f32[64,64]{1,0:T(8,128)S(1)} custom-call(f32[64,64]{1,0:T(8,128)S(1)} %fusion.48), custom_call_target="Cholesky" | custom-call | tf_op jit(solution)/shard_map/jit(cholesky)/cholesky | solution.py:69
  466.8 0.7 compare_reduce_fusion
  467.6 0.7 fusion.44
  468.3 4.9 custom-call.9
  473.2 0.3 fusion.46
  473.4 0.2 fusion.10
  473.6 5.0 fusion.1
  478.7 2.3 copy.58
  481.0 53.2 %all_to_all.33 = bf16[64,16,2048]{2,1,0:T(8,128)(2,1)S(1)} all-to-all(bf16[64,16,2048]{2,1,0:T(8,128)(2,1)S(1)} %copy.58), channel_id=1, replica_groups=mesh['mem'=16,'pix'=8] {'mem'}, dimensions={0} | all-to-all | bytes 8388608 | tf_op jit(solution)/shard_map/all_to_all | solution.py:34
  534.2 2.3 copy.72
  (20 shorter events, 0.2 us)
Async XLA Ops:
  74.6 7.8 %copy-start.4 = (s32[2,1200]{1,0:T(2,128)S(1)}, s32[2,1200]{1,0:T(2,128)}, u32[]{:S(2)}) copy-start(s32[2,1200]{1,0:T(2,128)} %param.13) | copy-start | bytes 28804
  74.6 7.9 %copy-start.6 = (s32[1200]{0:T(1024)S(1)}, s32[1200]{0:T(1024)}, u32[]{:S(2)}) copy-start(s32[1200]{0:T(1024)} %param.14) | copy-start | bytes 14404
  74.6 70.2 %all-to-all-start = ((bf16[16,2,65536]{2,1,0:T(2,128)(2,1)}), bf16[16,2,65536]{2,1,0:T(2,128)(2,1)}, u32[]{:S(2)}, u32[]{:S(2)}) async-start(bf16[16,2,65536]{2,1,0:T(2,128)(2,1)} %reshape.195), calls=%async_computation | async-start | bytes 8388608 | tf_op jit(solution)/shard_map/all_to_all | solution.py:29
  248.1 3.5 copy-start.1
  251.6 3.2 copy-start
  275.3 5.8 %copy-start.5 = (f32[1200]{0:T(1024)S(1)}, f32[1200]{0:T(1024)}, u32[]{:S(2)}) copy-start(f32[1200]{0:T(1024)} %param.11) | copy-start | bytes 14404
  275.3 6.3 %copy-start.9 = (f32[1200]{0:T(1024)S(1)}, f32[1200]{0:T(1024)}, u32[]{:S(2)}) copy-start(f32[1200]{0:T(1024)} %param.10) | copy-start | bytes 14404
  279.3 2.3 copy-start.7
  382.9 5.8 %copy-start.2 = (f32[64,16,2048]{2,0,1:T(8,128)S(1)}, f32[64,16,2048]{2,0,1:T(8,128)}, u32[]{:S(2)}) copy-start(f32[64,16,2048]{2,0,1:T(8,128)} %reshape.189) | copy-start | bytes 25165828
  390.1 2.3 copy-start.3
  394.0 2.2 copy-start.8
where the time goes:
time: 546 us; the launch traced here: 537 us
  local copies, waits for them, and re-layouts  232 us (42%)
  blocking collectives  183 us (34%)
  waiting for transfers between devices  62 us (11%)
  other arithmetic  33.1 us (6%)
  matrix products  17.5 us (3%)
  starting transfers between devices  7.76 us (1%)
    psum x2, blocking collectives, body(): gram, cross = lax.psum(products(scaled, misfit), ('mem', 'pix'))  130 us
    unnamed x25, local copies, waits for them, and re-layouts  116 us
    all_to_all x2, local copies, waits for them, and re-layouts, to_pixels(): lax.all_to_all(ground_motion_vector, 'mem', split_axis=2, concat_axis=0,...  77.7 us
    all_to_all x1, waiting for transfers between devices, to_pixels(): lax.all_to_all(ground_motion_vector, 'mem', split_axis=2, concat_axis=0,...  62 us
    all_to_all x1, blocking collectives, to_members(): lax.all_to_all(pixel_state, 'mem', split_axis=0, concat_axis=2, tiled=True)  53.2 us
    convert_element_type x3, local copies, waits for them, and re-layouts, update(): pixel_state.astype(jnp.float32) + change.reshape(pixel_state.shape)  30.9 us
    another operation x6, other arithmetic, solve_mixing(): jnp.linalg.cholesky(jnp.eye(realization_vectors, dtype=jnp.float32) + gram)  13.1 us
    another operation x4, other arithmetic, solve_mixing(): jax.scipy.linalg.cho_solve((factor, True), cross)  11.1 us
  transfers between devices with their start and end apart: 1, of which 1 were waited for; matrix products, arithmetic and copies ran while one was open for 0% of the time, Pallas kernels for 0%

commit v1 on v0

v1 whole, which is shorter than its diff:
```python
import functools
import math

import jax
import jax.numpy as jnp
from jax import lax
from jax.experimental import pallas as pl
from jax.experimental.pallas import tpu as pltpu
from jax.sharding import PartitionSpec as P

MESH = pl.DeviceIdType.MESH
HIGHEST = lax.Precision.HIGHEST
BLK = 64
PASS_COUNT = 2
MEMBERS = 64
TIMES = 16
NOBS = 1200
OBS = 1280
HALF = OBS // 2
OWN = 4
CELLS = 32768
PART = 2048
BLOCKS = CELLS // BLK
NPIX = 8
STEPS = 4
COLS = PART // STEPS
GROUP = 4
ROOT = math.sqrt(MEMBERS - 1)

ORDER = (
    (0, 1), (1, 0), (0, 3), (3, 0), (1, 1), (3, 3), (1, 3), (3, 1),
    (2, 2), (0, 2), (2, 0), (1, 2), (2, 1), (3, 2), (2, 3),
)
EARLY = 15


def iota(shape, axis):
    return lax.broadcasted_iota(jnp.int32, shape, axis)


def f32_dot(a, b, dims=((1,), (0,))):
    return lax.dot_general(a, b, (dims, ((), ())), precision=HIGHEST, preferred_element_type=jnp.float32)


def bf16_dot(a, b):
    return jnp.dot(a, b, preferred_element_type=jnp.float32)


def solve(system):
    row_at = iota(system.shape, 0)
    for start in range(0, MEMBERS, GROUP):
        columns = [jnp.broadcast_to(system[:, start + j : start + j + 1], system.shape) for j in range(GROUP)]
        for j in range(GROUP):
            k = start + j
            here = row_at == k
            inverse = 1.0 / columns[j][k : k + 1, :]
            pivot_row = system[k : k + 1, :] * inverse
            for later in range(j + 1, GROUP):
                share = columns[later][k : k + 1, :] * inverse
                columns[later] = jnp.where(here, share, columns[later] - columns[j] * share)
            system = jnp.where(here, pivot_row, system - columns[j] * pivot_row)
    return system[:, MEMBERS:]


def kernel(
    prior, obs, jitter, out,
    own, received, result, spread, noise, part_pred, pix_pred, whole_pred, mem_pred, predicted,
    load_sem, noise_sem, self_sem, put_sem,
    send_sem, recv_sem, pix_send, pix_recv, mem_send, mem_recv, back_send, back_recv,
):
    mem = lax.axis_index("mem")
    pix = lax.axis_index("pix")
    y = mem // 4
    x = mem % 4
    partners = [(((y + dy) % 4) * 4 + (x + dx) % 4) for dy, dx in ORDER]
    lines = [(pix + d) % NPIX for d in range(1, NPIX)]

    barrier = pltpu.get_barrier_semaphore()
    for p in partners:
        pl.semaphore_signal(barrier, 1, device_id=(p, pix), device_id_type=MESH)
    for p in lines:
        pl.semaphore_signal(barrier, 1, device_id=(mem, p), device_id_type=MESH)

    load = pltpu.make_async_copy(prior, own, load_sem)
    load.start()
    mine = pltpu.make_async_copy(
        prior.at[:, :, pl.ds(pl.multiple_of(mem * PART, PART), PART)],
        received.at[pl.ds(OWN * mem, OWN)],
        self_sem,
    )
    mine.start()
    noises = [pltpu.make_async_copy(jitter.at[i], noise.at[i, pl.ds(0, NOBS)], noise_sem.at[i]) for i in range(PASS_COUNT)]
    for copy in noises:
        copy.start()
    for i in range(PASS_COUNT):
        noise[i, NOBS:, :] = jnp.zeros((OBS - NOBS, MEMBERS), jnp.float32)

    pl.semaphore_wait(barrier, len(partners) + len(lines))

    def outgoing(s, i):
        p = partners[i]
        return pltpu.make_async_remote_copy(
            prior.at[pl.ds(s, 1), :, pl.ds(pl.multiple_of(p * PART, PART), PART)],
            received.at[pl.ds(OWN * mem + s, 1)],
            send_sem.at[s, i],
            recv_sem.at[s, i],
            device_id=(p, pix),
            device_id_type=MESH,
        )

    outgoings = [outgoing(s, i) for s in range(OWN) for i in range(len(ORDER))]
    for copy in outgoings[:EARLY]:
        copy.start()

    load.wait()
    depth = 1024

    def add_blocks(step, total):
        ones = jnp.where(iota((depth, 128), 1) - (iota((depth, 128), 0) >> 6) == step * (depth // BLK), 1.0, 0.0)
        rows = [
            own[:, :, pl.ds(pl.multiple_of(c * 8192 + step * depth, depth), depth)].reshape(OWN * TIMES, depth)
            for c in range(4)
        ]
        return total + bf16_dot(jnp.concatenate(rows, axis=0), ones.astype(jnp.bfloat16))

    sums = lax.fori_loop(0, 8192 // depth, add_blocks, jnp.zeros((4 * OWN * TIMES, 128), jnp.float32))
    sums = jnp.concatenate([sums[c * 64 : (c + 1) * 64] for c in range(4)], axis=1)
    high = sums.astype(jnp.bfloat16)
    rest = sums - high.astype(jnp.float32)
    middle = rest.astype(jnp.bfloat16)
    low = (rest - middle.astype(jnp.float32)).astype(jnp.bfloat16)
    parts = jnp.concatenate([high, middle, low], axis=0)

    for h in range(2):
        lanes = slice(h * HALF, (h + 1) * HALF)
        block = obs[2:3, lanes].astype(jnp.int32) - pix * BLOCKS
        pick = jnp.where(iota((BLOCKS, HALF), 0) == block, 1.0, 0.0).astype(jnp.bfloat16)
        seen = bf16_dot(parts, pick)
        seen = seen[0:64] + seen[64:128] + seen[128:192]
        scene = iota((TIMES, HALF), 0)
        pair = jnp.where(scene == obs[4:5, lanes].astype(jnp.int32), 1.0, 0.0) - jnp.where(
            scene == obs[3:4, lanes].astype(jnp.int32), 1.0, 0.0
        )
        part_pred[h * OWN : (h + 1) * OWN, :] = (
            jnp.sum(seen.reshape(OWN, TIMES, HALF) * pair[None], axis=1) * (1.0 / BLK)
        )

    line_copies = [
        pltpu.make_async_remote_copy(
            part_pred, pix_pred.at[pix], pix_send.at[d], pix_recv.at[d], device_id=(mem, p), device_id_type=MESH
        )
        for d, p in enumerate(lines)
    ]
    for copy in line_copies:
        copy.start()
    for copy in line_copies:
        copy.wait()
    whole = part_pred[...]
    for p in lines:
        whole = whole + pix_pred[p]
    whole_pred[...] = whole
    mem_pred[mem] = whole

    plane_copies = [
        pltpu.make_async_remote_copy(
            whole_pred, mem_pred.at[mem], mem_send.at[d], mem_recv.at[d], device_id=(p, pix), device_id_type=MESH
        )
        for d, p in enumerate(partners)
    ]
    for copy in plane_copies:
        copy.start()
    for copy in outgoings[EARLY:]:
        copy.start()
    for copy in noises:
        copy.wait()
    for copy in plane_copies:
        copy.wait()

    for s in range(16):
        for h in range(2):
            predicted[OWN * s : OWN * (s + 1), h * HALF : (h + 1) * HALF] = mem_pred[s, h * OWN : (h + 1) * OWN, :]

    error = obs[1:2, :] * math.sqrt(float(PASS_COUNT))
    pred = predicted[...]
    mean = jnp.sum(pred, axis=0, keepdims=True) * (1.0 / MEMBERS)
    scaled = (pred - mean) / (error * ROOT)
    offset = jnp.sum(scaled * ((obs[0:1, :] - mean) / error), axis=1, keepdims=True)
    gram = f32_dot(scaled, scaled, ((1,), (1,)))
    cross = [f32_dot(scaled, noise[i]) + offset for i in range(PASS_COUNT)]
    eye = jnp.where(iota((MEMBERS, MEMBERS), 0) == iota((MEMBERS, MEMBERS), 1), 1.0, 0.0)

    def rounded(solved):
        return (solved * (1.0 / ROOT)).astype(jnp.bfloat16).astype(jnp.float32)

    first = rounded(solve(jnp.concatenate([eye + gram, cross[0] - ROOT * gram], axis=1)))
    moved = f32_dot(gram, first)
    change = eye + first - jnp.mean(first, axis=1, keepdims=True)
    both = gram + moved
    right = jnp.concatenate([both - jnp.mean(moved, axis=1, keepdims=True), cross[1] - ROOT * both], axis=1)
    system = f32_dot(change.T, right)
    second = rounded(solve(system + jnp.concatenate([eye, jnp.zeros_like(eye)], axis=1)))
    one = first - jnp.mean(first, axis=0, keepdims=True)
    two = second - jnp.mean(second, axis=0, keepdims=True)
    total = one + two + f32_dot(one, two)

    widen = jnp.where(iota((MEMBERS, MEMBERS * TIMES), 1) >> 4 == iota((MEMBERS, MEMBERS * TIMES), 0), 1.0, 0.0)
    wide = bf16_dot(total.T.astype(jnp.bfloat16), widen.astype(jnp.bfloat16))
    same = (iota((TIMES, MEMBERS * TIMES), 1) & (TIMES - 1)) == iota((TIMES, MEMBERS * TIMES), 0)
    for j in range(MEMBERS):
        spread[j * TIMES : (j + 1) * TIMES, :] = jnp.where(same, wide[j : j + 1, :], 0.0).astype(jnp.bfloat16)

    mine.wait()
    for copy in outgoings:
        copy.wait()

    def incoming(step, i):
        p = partners[i]
        return pltpu.make_async_remote_copy(
            result.at[pl.ds(OWN * p, OWN), :, pl.ds(pl.multiple_of(step * COLS, COLS), COLS)],
            out.at[:, :, pl.ds(pl.multiple_of(mem * PART + step * COLS, COLS), COLS)],
            back_send.at[step, i],
            back_recv.at[step, i],
            device_id=(p, pix),
            device_id_type=MESH,
        )

    def keep(step):
        return pltpu.make_async_copy(
            result.at[pl.ds(OWN * mem, OWN), :, pl.ds(pl.multiple_of(step * COLS, COLS), COLS)],
            out.at[:, :, pl.ds(pl.multiple_of(mem * PART + step * COLS, COLS), COLS)],
            put_sem.at[step],
        )

    def advance(step, carry):
        lanes = pl.ds(pl.multiple_of(step * COLS, COLS), COLS)
        state = received[:, :, lanes].reshape(MEMBERS * TIMES, COLS)
        for r in range(4):
            members = slice(r * 16, (r + 1) * 16)
            rows = slice(r * 256, (r + 1) * 256)
            moved = bf16_dot(spread[rows, :], state)
            fresh = received[members, :, lanes].reshape(256, COLS).astype(jnp.float32) + moved
            result[members, :, lanes] = fresh.astype(jnp.bfloat16).reshape(16, TIMES, COLS)
        for i in range(len(ORDER)):
            incoming(step, i).start()
        keep(step).start()
        return carry

    lax.fori_loop(0, STEPS, advance, 0)

    def finish(step, carry):
        for i in range(len(ORDER)):
            incoming(step, i).wait()
        keep(step).wait()
        return carry

    lax.fori_loop(0, STEPS, finish, 0)


def body(prior_motion, measured_motion, measurement_noise_stddev, gaussian_jitter, scene_couples, targeted_tile_number):
    def row(values, fill):
        return jnp.pad(values.astype(jnp.float32), (0, OBS - NOBS), constant_values=fill)[None]

    obs = jnp.concatenate(
        [
            row(measured_motion, 0.0),
            row(measurement_noise_stddev, 1.0),
            row(targeted_tile_number, -1.0),
            row(scene_couples[0], 0.0),
            row(scene_couples[1], 0.0),
            jnp.zeros((3, OBS), jnp.float32),
        ],
        axis=0,
    )
    anywhere = pl.BlockSpec(memory_space=pl.ANY)
    dma = pltpu.SemaphoreType.DMA
    n = len(ORDER)
    return pl.pallas_call(
        kernel,
        out_shape=jax.ShapeDtypeStruct(prior_motion.shape, jnp.bfloat16),
        in_specs=[anywhere, pl.BlockSpec(memory_space=pltpu.VMEM), anywhere],
        out_specs=anywhere,
        scratch_shapes=[
            pltpu.VMEM((OWN, TIMES, CELLS), jnp.bfloat16),
            pltpu.VMEM((MEMBERS, TIMES, PART), jnp.bfloat16),
            pltpu.VMEM((MEMBERS, TIMES, PART), jnp.bfloat16),
            pltpu.VMEM((MEMBERS * TIMES, MEMBERS * TIMES), jnp.bfloat16),
            pltpu.VMEM((PASS_COUNT, OBS, MEMBERS), jnp.float32),
            pltpu.VMEM((2 * OWN, HALF), jnp.float32),
            pltpu.VMEM((NPIX, 2 * OWN, HALF), jnp.float32),
            pltpu.VMEM((2 * OWN, HALF), jnp.float32),
            pltpu.VMEM((16, 2 * OWN, HALF), jnp.float32),
            pltpu.VMEM((MEMBERS, OBS), jnp.float32),
            dma, dma((PASS_COUNT,)), dma, dma((STEPS,)),
            dma((OWN, n)), dma((OWN, n)),
            dma((NPIX - 1,)), dma((NPIX - 1,)),
            dma((n,)), dma((n,)),
            dma((STEPS, n)), dma((STEPS, n)),
        ],
        compiler_params=pltpu.CompilerParams(collective_id=0, has_side_effects=True, vmem_limit_bytes=60 << 20),
        name="smoother",
    )(prior_motion, obs, gaussian_jitter)


def solution(mesh):
    return jax.shard_map(
        body,
        mesh=mesh,
        in_specs=(P("mem", None, "pix"), P(), P(), P(), P(), P()),
        out_specs=P("mem", None, "pix"),
        check_vma=False,
    )
```

time: 546 us -> 123 us (0.23); the launches traced: 537 us -> 123 us
  local copies, waits for them, and re-layouts: 232 us -> 9.1 us
  blocking collectives: 183 us -> 0 us
  Pallas kernels: 0 us -> 112 us
  waiting for transfers between devices: 62 us -> 0 us
  other arithmetic: 33.1 us -> 1.51 us
  matrix products: 17.5 us -> 0 us
  starting transfers between devices: 7.76 us -> 0 us
    psum x2 -> x0, blocking collectives: 130 us -> none  [body(): gram, cross = lax.psum(products(scaled, misfit), ('mem', 'pix'))]
    pallas_call x0 -> x1, Pallas kernels: none -> 112 us  [body(): pl.pallas_call(kernel, out_shape=jax.ShapeDtypeStruct(prior_motion.shape,...]
    unnamed x25 -> x2, local copies, waits for them, and re-layouts: 116 us -> 6.98 us
    all_to_all x3 -> x0, local copies, waits for them, and re-layouts: 80 us -> none  [the longest x2 77.7 us: to_pixels(): lax.all_to_all(ground_motion_vector, 'mem', split_axis=2, concat_axis=0,...]
    all_to_all x1 -> x0, waiting for transfers between devices: 62 us -> none  [to_pixels(): lax.all_to_all(ground_motion_vector, 'mem', split_axis=2, concat_axis=0,...]
    all_to_all x1 -> x0, blocking collectives: 53.2 us -> none  [to_members(): lax.all_to_all(pixel_state, 'mem', split_axis=0, concat_axis=2, tiled=True)]
    convert_element_type x5 -> x0, local copies, waits for them, and re-layouts: 35.5 us -> none  [the longest x3 30.9 us: update(): pixel_state.astype(jnp.float32) + change.reshape(pixel_state.shape)]
    another operation x10 -> x0, other arithmetic: 24.3 us -> none  [the longest x6 13.1 us: solve_mixing(): jnp.linalg.cholesky(jnp.eye(realization_vectors, dtype=jnp.float32) + gram)]
  transfers between devices with their start and end apart: 1 -> 0, of which waited for: 1 -> 0; matrix products, arithmetic and copies ran while one was open for 0% -> 0% of each run, Pallas kernels for 0% -> 0%
where the time goes in v1:
time: 123 us
  Pallas kernels  112 us (91%)
  local copies, waits for them, and re-layouts  9.1 us (7%)
  other arithmetic  1.51 us (1%)
    pallas_call x1, Pallas kernels, body(): pl.pallas_call(kernel, out_shape=jax.ShapeDtypeStruct(prior_motion.shape,...  112 us
    unnamed x2, local copies, waits for them, and re-layouts  6.98 us

profile of v1, /device:TPU:1, one launch (start us, length us, event | category | flops | bytes accessed | tf_op | source)
XLA Modules:
  0.0 122.9 jit_solution(7930138095032552583)
XLA Ops:
  0.0 0.7 pad.16
  0.7 0.7 pad.17
  1.4 0.7 convert_element_type.15
  2.1 0.8 convert_reduce_fusion
  3.0 0.7 concatenate.3.obs
  3.7 2.5 %copy.7.jitter = f32[2,1200,64]{2,1,0:T(8,128)} copy(f32[2,1200,64]{1,2,0:T(8,128)} %param.9) | data formatting | bytes 1228800 | tf_op args[3]
  6.2 112.3 %smoother.1 = bf16[4,16,32768]{2,1,0:T(8,128)(2,1)} custom-call(bf16[4,16,32768]{2,1,0:T(8,128)(2,1)} %prior.1, f32[8,1280]{1,0:T(8,128)} %concatenate.3.obs, f32[2,1200,64]{2,1,0:T(8,128)} %copy.7.jitter), custom_call_target="tpu_custom_call" | custom-call | tf_op jit(solution)/shard_map/smoother/pallas_call | solution.py:277
  118.4 4.5 %copy.9 = bf16[4,16,32768]{2,1,0:T(8,128)(2,1)} copy(bf16[4,16,32768]{2,1,0:T(8,128)(2,1)} %smoother.1) | data formatting | bytes 8388608
  (9 shorter events, 0.0 us)

commit v2 on v1

--- a/solution.py
+++ b/solution.py
@@ -31,7 +31,7 @@
     (0, 1), (1, 0), (0, 3), (3, 0), (1, 1), (3, 3), (1, 3), (3, 1),
     (2, 2), (0, 2), (2, 0), (1, 2), (2, 1), (3, 2), (2, 3),
 )
-EARLY = 15
+EARLY = 30
 
 
 def iota(shape, axis):
@@ -63,9 +63,10 @@
 
 
 def kernel(
-    prior, obs, jitter, out,
-    own, received, result, spread, noise, part_pred, pix_pred, whole_pred, mem_pred, predicted,
-    load_sem, noise_sem, self_sem, put_sem,
+    prior, measured, stddev, jitter, couples, tiles, out,
+    own, received, result, spread, keeps, noise, pairs, table,
+    part_pred, pix_pred, whole_pred, mem_pred, predicted,
+    load_sem, small_sem, self_sem,
     send_sem, recv_sem, pix_send, pix_recv, mem_send, mem_recv, back_send, back_recv,
 ):
     mem = lax.axis_index("mem")
@@ -89,26 +90,33 @@
         self_sem,
     )
     mine.start()
-    noises = [pltpu.make_async_copy(jitter.at[i], noise.at[i, pl.ds(0, NOBS)], noise_sem.at[i]) for i in range(PASS_COUNT)]
-    for copy in noises:
-        copy.start()
-    for i in range(PASS_COUNT):
-        noise[i, NOBS:, :] = jnp.zeros((OBS - NOBS, MEMBERS), jnp.float32)
+    smalls = [
+        pltpu.make_async_copy(src, dst, small_sem.at[i])
+        for i, (src, dst) in enumerate(
+            ((couples, pairs), (jitter, noise))
+        )
+    ]
+    for copy in smalls:
+        copy.start()
+    table[...] = jnp.full(table.shape, -1, jnp.int32)
 
     pl.semaphore_wait(barrier, len(partners) + len(lines))
+
+    def columns(start, step):
+        return pl.ds(pl.multiple_of(start * PART + step * COLS, COLS), COLS)
 
     def outgoing(s, i):
         p = partners[i]
         return pltpu.make_async_remote_copy(
-            prior.at[pl.ds(s, 1), :, pl.ds(pl.multiple_of(p * PART, PART), PART)],
-            received.at[pl.ds(OWN * mem + s, 1)],
+            prior.at[:, :, columns(p, s)],
+            received.at[pl.ds(OWN * mem, OWN), :, pl.ds(s * COLS, COLS)],
             send_sem.at[s, i],
             recv_sem.at[s, i],
             device_id=(p, pix),
             device_id_type=MESH,
         )
 
-    outgoings = [outgoing(s, i) for s in range(OWN) for i in range(len(ORDER))]
+    outgoings = [outgoing(s, i) for s in range(STEPS) for i in range(len(ORDER))]
     for copy in outgoings[:EARLY]:
         copy.start()
 
@@ -131,15 +139,19 @@
     low = (rest - middle.astype(jnp.float32)).astype(jnp.bfloat16)
     parts = jnp.concatenate([high, middle, low], axis=0)
 
+    smalls[0].wait()
+    table[0:2, 0:NOBS] = pairs[...]
+    table[2:3, 0:NOBS] = tiles[...].reshape(1, NOBS)
+
     for h in range(2):
         lanes = slice(h * HALF, (h + 1) * HALF)
-        block = obs[2:3, lanes].astype(jnp.int32) - pix * BLOCKS
+        block = table[2:3, lanes] - pix * BLOCKS
         pick = jnp.where(iota((BLOCKS, HALF), 0) == block, 1.0, 0.0).astype(jnp.bfloat16)
         seen = bf16_dot(parts, pick)
         seen = seen[0:64] + seen[64:128] + seen[128:192]
         scene = iota((TIMES, HALF), 0)
-        pair = jnp.where(scene == obs[4:5, lanes].astype(jnp.int32), 1.0, 0.0) - jnp.where(
-            scene == obs[3:4, lanes].astype(jnp.int32), 1.0, 0.0
+        pair = jnp.where(scene == table[1:2, lanes], 1.0, 0.0) - jnp.where(
+            scene == table[0:1, lanes], 1.0, 0.0
         )
         part_pred[h * OWN : (h + 1) * OWN, :] = (
             jnp.sum(seen.reshape(OWN, TIMES, HALF) * pair[None], axis=1) * (1.0 / BLK)
@@ -171,8 +183,7 @@
         copy.start()
     for copy in outgoings[EARLY:]:
         copy.start()
-    for copy in noises:
-        copy.wait()
+    smalls[1].wait()
     for copy in plane_copies:
         copy.wait()
 
@@ -180,13 +191,13 @@
         for h in range(2):
             predicted[OWN * s : OWN * (s + 1), h * HALF : (h + 1) * HALF] = mem_pred[s, h * OWN : (h + 1) * OWN, :]
 
-    error = obs[1:2, :] * math.sqrt(float(PASS_COUNT))
-    pred = predicted[...]
+    scale = stddev[...].reshape(1, NOBS) * math.sqrt(float(PASS_COUNT))
+    pred = predicted[:, 0:NOBS]
     mean = jnp.sum(pred, axis=0, keepdims=True) * (1.0 / MEMBERS)
-    scaled = (pred - mean) / (error * ROOT)
-    offset = jnp.sum(scaled * ((obs[0:1, :] - mean) / error), axis=1, keepdims=True)
+    scaled = (pred - mean) / (scale * ROOT)
+    offset = jnp.sum(scaled * ((measured[...].reshape(1, NOBS) - mean) / scale), axis=1, keepdims=True)
     gram = f32_dot(scaled, scaled, ((1,), (1,)))
-    cross = [f32_dot(scaled, noise[i]) + offset for i in range(PASS_COUNT)]
+    cross = [f32_dot(scaled, noise[i], ((1,), (1,))) + offset for i in range(PASS_COUNT)]
     eye = jnp.where(iota((MEMBERS, MEMBERS), 0) == iota((MEMBERS, MEMBERS), 1), 1.0, 0.0)
 
     def rounded(solved):
@@ -202,47 +213,45 @@
     one = first - jnp.mean(first, axis=0, keepdims=True)
     two = second - jnp.mean(second, axis=0, keepdims=True)
     total = one + two + f32_dot(one, two)
+    own_share = jnp.sum(total * eye, axis=1, keepdims=True)
+    factor = jnp.broadcast_to(own_share + 1.0, (MEMBERS, 128))
+    total = total - own_share * eye
 
     widen = jnp.where(iota((MEMBERS, MEMBERS * TIMES), 1) >> 4 == iota((MEMBERS, MEMBERS * TIMES), 0), 1.0, 0.0)
     wide = bf16_dot(total.T.astype(jnp.bfloat16), widen.astype(jnp.bfloat16))
     same = (iota((TIMES, MEMBERS * TIMES), 1) & (TIMES - 1)) == iota((TIMES, MEMBERS * TIMES), 0)
     for j in range(MEMBERS):
         spread[j * TIMES : (j + 1) * TIMES, :] = jnp.where(same, wide[j : j + 1, :], 0.0).astype(jnp.bfloat16)
+        keeps[j * TIMES : (j + 1) * TIMES, :] = jnp.broadcast_to(factor[j : j + 1, :], (TIMES, 128))
 
     mine.wait()
-    for copy in outgoings:
-        copy.wait()
 
     def incoming(step, i):
         p = partners[i]
         return pltpu.make_async_remote_copy(
-            result.at[pl.ds(OWN * p, OWN), :, pl.ds(pl.multiple_of(step * COLS, COLS), COLS)],
-            out.at[:, :, pl.ds(pl.multiple_of(mem * PART + step * COLS, COLS), COLS)],
+            result.at[pl.ds(OWN * p, OWN), :, columns(0, step)],
+            out.at[:, :, columns(mem, step)],
             back_send.at[step, i],
             back_recv.at[step, i],
             device_id=(p, pix),
             device_id_type=MESH,
         )
 
-    def keep(step):
-        return pltpu.make_async_copy(
-            result.at[pl.ds(OWN * mem, OWN), :, pl.ds(pl.multiple_of(step * COLS, COLS), COLS)],
-            out.at[:, :, pl.ds(pl.multiple_of(mem * PART + step * COLS, COLS), COLS)],
-            put_sem.at[step],
-        )
-
     def advance(step, carry):
-        lanes = pl.ds(pl.multiple_of(step * COLS, COLS), COLS)
+        for i in range(len(ORDER)):
+            outgoing(step, i).wait()
+        lanes = columns(0, step)
         state = received[:, :, lanes].reshape(MEMBERS * TIMES, COLS)
         for r in range(4):
             members = slice(r * 16, (r + 1) * 16)
             rows = slice(r * 256, (r + 1) * 256)
             moved = bf16_dot(spread[rows, :], state)
-            fresh = received[members, :, lanes].reshape(256, COLS).astype(jnp.float32) + moved
-            result[members, :, lanes] = fresh.astype(jnp.bfloat16).reshape(16, TIMES, COLS)
+            kept = received[members, :, lanes].reshape(256, COLS).astype(jnp.float32)
+            factors = jnp.concatenate([keeps[rows, :]] * (COLS // 128), axis=1)
+            result[members, :, lanes] = (kept * factors + moved).astype(jnp.bfloat16).reshape(16, TIMES, COLS)
         for i in range(len(ORDER)):
             incoming(step, i).start()
-        keep(step).start()
+        out[:, :, columns(mem, step)] = result[pl.ds(OWN * mem, OWN), :, lanes]
         return carry
 
     lax.fori_loop(0, STEPS, advance, 0)
@@ -250,55 +259,51 @@
     def finish(step, carry):
         for i in range(len(ORDER)):
             incoming(step, i).wait()
-        keep(step).wait()
         return carry
 
     lax.fori_loop(0, STEPS, finish, 0)
 
 
 def body(prior_motion, measured_motion, measurement_noise_stddev, gaussian_jitter, scene_couples, targeted_tile_number):
-    def row(values, fill):
-        return jnp.pad(values.astype(jnp.float32), (0, OBS - NOBS), constant_values=fill)[None]
-
-    obs = jnp.concatenate(
-        [
-            row(measured_motion, 0.0),
-            row(measurement_noise_stddev, 1.0),
-            row(targeted_tile_number, -1.0),
-            row(scene_couples[0], 0.0),
-            row(scene_couples[1], 0.0),
-            jnp.zeros((3, OBS), jnp.float32),
-        ],
-        axis=0,
-    )
-    anywhere = pl.BlockSpec(memory_space=pl.ANY)
+    anywhere = pl.BlockSpec(memory_space=pltpu.HBM)
+    small = pl.BlockSpec(memory_space=pltpu.VMEM)
     dma = pltpu.SemaphoreType.DMA
     n = len(ORDER)
     return pl.pallas_call(
         kernel,
-        out_shape=jax.ShapeDtypeStruct(prior_motion.shape, jnp.bfloat16),
-        in_specs=[anywhere, pl.BlockSpec(memory_space=pltpu.VMEM), anywhere],
-        out_specs=anywhere,
+        out_shape=pltpu.VMEM(prior_motion.shape, jnp.bfloat16),
+        in_specs=[anywhere, small, small, anywhere, anywhere, small],
+        out_specs=pl.BlockSpec(memory_space=pltpu.VMEM),
         scratch_shapes=[
             pltpu.VMEM((OWN, TIMES, CELLS), jnp.bfloat16),
             pltpu.VMEM((MEMBERS, TIMES, PART), jnp.bfloat16),
             pltpu.VMEM((MEMBERS, TIMES, PART), jnp.bfloat16),
             pltpu.VMEM((MEMBERS * TIMES, MEMBERS * TIMES), jnp.bfloat16),
-            pltpu.VMEM((PASS_COUNT, OBS, MEMBERS), jnp.float32),
+            pltpu.VMEM((MEMBERS * TIMES, 128), jnp.float32),
+            pltpu.VMEM((PASS_COUNT, MEMBERS, NOBS), jnp.float32),
+            pltpu.VMEM((2, NOBS), jnp.int32),
+            pltpu.VMEM((8, OBS), jnp.int32),
             pltpu.VMEM((2 * OWN, HALF), jnp.float32),
             pltpu.VMEM((NPIX, 2 * OWN, HALF), jnp.float32),
             pltpu.VMEM((2 * OWN, HALF), jnp.float32),
             pltpu.VMEM((16, 2 * OWN, HALF), jnp.float32),
             pltpu.VMEM((MEMBERS, OBS), jnp.float32),
-            dma, dma((PASS_COUNT,)), dma, dma((STEPS,)),
-            dma((OWN, n)), dma((OWN, n)),
+            dma, dma((2,)), dma,
+            dma((STEPS, n)), dma((STEPS, n)),
             dma((NPIX - 1,)), dma((NPIX - 1,)),
             dma((n,)), dma((n,)),
             dma((STEPS, n)), dma((STEPS, n)),
         ],
-        compiler_params=pltpu.CompilerParams(collective_id=0, has_side_effects=True, vmem_limit_bytes=60 << 20),
+        compiler_params=pltpu.CompilerParams(collective_id=0, has_side_effects=True, vmem_limit_bytes=59 << 20),
         name="smoother",
-    )(prior_motion, obs, gaussian_jitter)
+    )(
+        prior_motion,
+        measured_motion,
+        measurement_noise_stddev,
+        jnp.swapaxes(gaussian_jitter, 1, 2),
+        scene_couples,
+        targeted_tile_number,
+    )
 
 
 def solution(mesh):

time: 123 us -> 110 us (0.89)
  local copies, waits for them, and re-layouts: 9.1 us -> 2.02 us
  Pallas kernels: 112 us -> 108 us
  other arithmetic: 1.51 us -> 0 us
    unnamed x2 -> x1, local copies, waits for them, and re-layouts: 6.98 us -> 2.02 us
    pallas_call x1, Pallas kernels: 112 us -> 108 us  [body(): pl.pallas_call(kernel, out_shape=pltpu.VMEM(prior_motion.shape, jnp.bfloa...]
    convert_element_type x2 -> x0, other arithmetic: 1.51 us -> none  [row(): values.astype(jnp.float32)]
    pad x5 -> x0, local copies, waits for them, and re-layouts: 1.42 us -> none  [row(): jnp.pad(values.astype(jnp.float32), (0, OBS - NOBS), constant_values=fill)]
where the time goes in v2:
time: 110 us
  Pallas kernels  108 us (98%)
  local copies, waits for them, and re-layouts  2.02 us (2%)
    pallas_call x1, Pallas kernels, body(): pl.pallas_call(kernel, out_shape=pltpu.VMEM(prior_motion.shape, jnp.bfloa...  108 us

profile of v2, /device:TPU:1, one launch (start us, length us, event | category | flops | bytes accessed | tf_op | source)
XLA Modules:
  0.0 109.7 jit_solution(9260583829048270856)
XLA Ops:
  0.0 107.7 %smoother.1 = bf16[4,16,32768]{2,1,0:T(8,128)(2,1)S(1)} custom-call(bf16[4,16,32768]{2,1,0:T(8,128)(2,1)} %prior.1, f32[1200]{0:T(1024)} %measured.1, f32[1200]{0:T(1024)} %stddev.1, f32[2,64,1200]{2,1,0:T(8,128)} %bitcast.1, s32[2,1200]{1,0:T(2,128)} %couples.1, s32[1200]{0:T(1024)} %tiles.1), custom_call_target="tpu_custom_call" | custom-call | tf_op jit(solution)/shard_map/smoother/pallas_call | solution.py:272
  107.7 2.0 %copy.8 = bf16[4,16,32768]{2,1,0:T(8,128)(2,1)} copy(bf16[4,16,32768]{2,1,0:T(8,128)(2,1)S(1)} %smoother.1) | data formatting | bytes 8388608

commit v3 on v2

--- a/solution.py
+++ b/solution.py
@@ -15,13 +15,15 @@
 MEMBERS = 64
 TIMES = 16
 NOBS = 1200
-OBS = 1280
-HALF = OBS // 2
+CHUNK = 256
+CHUNKS = -(-NOBS // CHUNK)
 OWN = 4
 CELLS = 32768
 PART = 2048
 BLOCKS = CELLS // BLK
 NPIX = 8
+NZ = NPIX // 2
+OBS = NPIX * CHUNK
 STEPS = 4
 COLS = PART // STEPS
 GROUP = 4
@@ -64,10 +66,10 @@
 
 def kernel(
     prior, measured, stddev, jitter, couples, tiles, out,
-    own, received, result, spread, keeps, noise, pairs, table,
-    part_pred, pix_pred, whole_pred, mem_pred, predicted,
-    load_sem, small_sem, self_sem,
-    send_sem, recv_sem, pix_send, pix_recv, mem_send, mem_recv, back_send, back_recv,
+    own, received, result, spread, keeps, noise, padded_noise, levels, pairs, table,
+    part_pred, pix_pred, whole_pred, mem_pred, predicted, part_sum, twin_sum, line_sum,
+    load_sem, small_sem, self_sem, twin_send, twin_recv,
+    send_sem, recv_sem, pix_send, pix_recv, mem_send, mem_recv, line_send, line_recv, back_send, back_recv,
 ):
     mem = lax.axis_index("mem")
     pix = lax.axis_index("pix")
@@ -99,6 +101,12 @@
     for copy in smalls:
         copy.start()
     table[...] = jnp.full(table.shape, -1, jnp.int32)
+    part_pred[...] = jnp.zeros(part_pred.shape, jnp.float32)
+    padded_noise[:, :, 1152:] = jnp.zeros((PASS_COUNT, MEMBERS, OBS - 1152), jnp.float32)
+    levels[0:1, :] = jnp.zeros((1, OBS), jnp.float32)
+    levels[1:2, :] = jnp.ones((1, OBS), jnp.float32)
+    levels[0:1, 0:NOBS] = measured[...].reshape(1, NOBS)
+    levels[1:2, 0:NOBS] = stddev[...].reshape(1, NOBS)
 
     pl.semaphore_wait(barrier, len(partners) + len(lines))
 
@@ -143,23 +151,20 @@
     table[0:2, 0:NOBS] = pairs[...]
     table[2:3, 0:NOBS] = tiles[...].reshape(1, NOBS)
 
-    for h in range(2):
-        lanes = slice(h * HALF, (h + 1) * HALF)
-        block = table[2:3, lanes] - pix * BLOCKS
-        pick = jnp.where(iota((BLOCKS, HALF), 0) == block, 1.0, 0.0).astype(jnp.bfloat16)
-        seen = bf16_dot(parts, pick)
+    for q in range(CHUNKS):
+        lanes = slice(q * CHUNK, (q + 1) * CHUNK)
+        pick = jnp.where(iota((BLOCKS, CHUNK), 0) == table[2:3, lanes] - pix * BLOCKS, 1.0, 0.0)
+        seen = bf16_dot(parts, pick.astype(jnp.bfloat16))
         seen = seen[0:64] + seen[64:128] + seen[128:192]
-        scene = iota((TIMES, HALF), 0)
-        pair = jnp.where(scene == table[1:2, lanes], 1.0, 0.0) - jnp.where(
-            scene == table[0:1, lanes], 1.0, 0.0
-        )
-        part_pred[h * OWN : (h + 1) * OWN, :] = (
-            jnp.sum(seen.reshape(OWN, TIMES, HALF) * pair[None], axis=1) * (1.0 / BLK)
-        )
+        scene = iota((TIMES, CHUNK), 0)
+        pair = jnp.where(scene == table[1:2, lanes], 1.0, 0.0) - jnp.where(scene == table[0:1, lanes], 1.0, 0.0)
+        shift = jnp.sum(seen.reshape(OWN, TIMES, CHUNK) * pair[None], axis=1) * (1.0 / BLK)
+        part_pred[q, 0:OWN, :] = shift[:, 0:128]
+        part_pred[q, OWN:, :] = shift[:, 128:]
 
     line_copies = [
         pltpu.make_async_remote_copy(
-            part_pred, pix_pred.at[pix], pix_send.at[d], pix_recv.at[d], device_id=(mem, p), device_id_type=MESH
+            part_pred.at[p], pix_pred.at[pix], pix_send.at[d], pix_recv.at[d], device_id=(mem, p), device_id_type=MESH
         )
         for d, p in enumerate(lines)
     ]
@@ -167,7 +172,7 @@
         copy.start()
     for copy in line_copies:
         copy.wait()
-    whole = part_pred[...]
+    whole = part_pred[pix]
     for p in lines:
         whole = whole + pix_pred[p]
     whole_pred[...] = whole
@@ -184,20 +189,47 @@
     for copy in outgoings[EARLY:]:
         copy.start()
     smalls[1].wait()
+    padded_noise[:, :, 0:NOBS] = noise[...]
     for copy in plane_copies:
         copy.wait()
 
     for s in range(16):
-        for h in range(2):
-            predicted[OWN * s : OWN * (s + 1), h * HALF : (h + 1) * HALF] = mem_pred[s, h * OWN : (h + 1) * OWN, :]
-
-    scale = stddev[...].reshape(1, NOBS) * math.sqrt(float(PASS_COUNT))
-    pred = predicted[:, 0:NOBS]
+        predicted[OWN * s : OWN * (s + 1), 0:128] = mem_pred[s, 0:OWN, :]
+        predicted[OWN * s : OWN * (s + 1), 128:] = mem_pred[s, OWN:, :]
+
+    chunk = pl.ds(pl.multiple_of(pix * CHUNK, CHUNK), CHUNK)
+    scale = levels[1:2, chunk] * math.sqrt(float(PASS_COUNT))
+    pred = predicted[...]
     mean = jnp.sum(pred, axis=0, keepdims=True) * (1.0 / MEMBERS)
     scaled = (pred - mean) / (scale * ROOT)
-    offset = jnp.sum(scaled * ((measured[...].reshape(1, NOBS) - mean) / scale), axis=1, keepdims=True)
+    offset = jnp.sum(scaled * ((levels[0:1, chunk] - mean) / scale), axis=1, keepdims=True)
     gram = f32_dot(scaled, scaled, ((1,), (1,)))
-    cross = [f32_dot(scaled, noise[i], ((1,), (1,))) + offset for i in range(PASS_COUNT)]
+    cross = [f32_dot(scaled, padded_noise[i, :, chunk], ((1,), (1,))) + offset for i in range(PASS_COUNT)]
+    part_sum[0:64, :] = jnp.concatenate([gram, cross[0]], axis=1)
+    part_sum[64:96, :] = jnp.concatenate([cross[1][0:32], cross[1][32:64]], axis=1)
+
+    core = pix % 2
+    z = pix // 2
+    twin = pltpu.make_async_remote_copy(
+        part_sum, twin_sum, twin_send, twin_recv, device_id=(mem, z * 2 + 1 - core), device_id_type=MESH
+    )
+    twin.start()
+    twin.wait()
+    line_sum[z] = part_sum[...] + twin_sum[...]
+    sum_copies = [
+        pltpu.make_async_remote_copy(
+            line_sum.at[z], line_sum.at[z], line_send.at[d], line_recv.at[d],
+            device_id=(mem, ((z + 1 + d) % NZ) * 2 + core), device_id_type=MESH,
+        )
+        for d in range(NZ - 1)
+    ]
+    for copy in sum_copies:
+        copy.start()
+    for copy in sum_copies:
+        copy.wait()
+    products = line_sum[0] + line_sum[1] + line_sum[2] + line_sum[3]
+    gram = products[0:64, 0:64]
+    cross = [products[0:64, 64:128], jnp.concatenate([products[64:96, 0:64], products[64:96, 64:128]], axis=0)]
     eye = jnp.where(iota((MEMBERS, MEMBERS), 0) == iota((MEMBERS, MEMBERS), 1), 1.0, 0.0)
 
     def rounded(solved):
@@ -281,17 +313,23 @@
             pltpu.VMEM((MEMBERS * TIMES, MEMBERS * TIMES), jnp.bfloat16),
             pltpu.VMEM((MEMBERS * TIMES, 128), jnp.float32),
             pltpu.VMEM((PASS_COUNT, MEMBERS, NOBS), jnp.float32),
+            pltpu.VMEM((PASS_COUNT, MEMBERS, OBS), jnp.float32),
+            pltpu.VMEM((8, OBS), jnp.float32),
             pltpu.VMEM((2, NOBS), jnp.int32),
             pltpu.VMEM((8, OBS), jnp.int32),
-            pltpu.VMEM((2 * OWN, HALF), jnp.float32),
-            pltpu.VMEM((NPIX, 2 * OWN, HALF), jnp.float32),
-            pltpu.VMEM((2 * OWN, HALF), jnp.float32),
-            pltpu.VMEM((16, 2 * OWN, HALF), jnp.float32),
-            pltpu.VMEM((MEMBERS, OBS), jnp.float32),
-            dma, dma((2,)), dma,
+            pltpu.VMEM((NPIX, 2 * OWN, 128), jnp.float32),
+            pltpu.VMEM((NPIX, 2 * OWN, 128), jnp.float32),
+            pltpu.VMEM((2 * OWN, 128), jnp.float32),
+            pltpu.VMEM((16, 2 * OWN, 128), jnp.float32),
+            pltpu.VMEM((MEMBERS, CHUNK), jnp.float32),
+            pltpu.VMEM((96, 128), jnp.float32),
+            pltpu.VMEM((96, 128), jnp.float32),
+            pltpu.VMEM((NZ, 96, 128), jnp.float32),
+            dma, dma((2,)), dma, dma, dma,
             dma((STEPS, n)), dma((STEPS, n)),
             dma((NPIX - 1,)), dma((NPIX - 1,)),
             dma((n,)), dma((n,)),
+            dma((NZ - 1,)), dma((NZ - 1,)),
             dma((STEPS, n)), dma((STEPS, n)),
         ],
         compiler_params=pltpu.CompilerParams(collective_id=0, has_side_effects=True, vmem_limit_bytes=59 << 20),

time: 110 us -> 107 us (0.973)
  Pallas kernels: 108 us -> 105 us
    pallas_call x1, Pallas kernels: 108 us -> 105 us  [body(): pl.pallas_call(kernel, out_shape=pltpu.VMEM(prior_motion.shape, jnp.bfloa...]
where the time goes in v3:
time: 107 us
  Pallas kernels  105 us (98%)
  local copies, waits for them, and re-layouts  2.02 us (2%)
    pallas_call x1, Pallas kernels, body(): pl.pallas_call(kernel, out_shape=pltpu.VMEM(prior_motion.shape, jnp.bfloa...  105 us

profile of v3, /device:TPU:1, one launch (start us, length us, event | category | flops | bytes accessed | tf_op | source)
XLA Modules:
  0.0 106.9 jit_solution(18090511053707572477)
XLA Ops:
  0.0 104.9 %smoother.1 = bf16[4,16,32768]{2,1,0:T(8,128)(2,1)S(1)} custom-call(bf16[4,16,32768]{2,1,0:T(8,128)(2,1)} %prior.1, f32[1200]{0:T(1024)} %measured.1, f32[1200]{0:T(1024)} %stddev.1, f32[2,64,1200]{2,1,0:T(8,128)} %bitcast.1, s32[2,1200]{1,0:T(2,128)} %couples.1, s32[1200]{0:T(1024)} %tiles.1), custom_call_target="tpu_custom_call" | custom-call | tf_op jit(solution)/shard_map/smoother/pallas_call | solution.py:304
  104.9 2.0 %copy.8 = bf16[4,16,32768]{2,1,0:T(8,128)(2,1)} copy(bf16[4,16,32768]{2,1,0:T(8,128)(2,1)S(1)} %smoother.1) | data formatting | bytes 8388608

commit v4 on v3

--- a/solution.py
+++ b/solution.py
@@ -75,7 +75,10 @@
     pix = lax.axis_index("pix")
     y = mem // 4
     x = mem % 4
-    partners = [(((y + dy) % 4) * 4 + (x + dx) % 4) for dy, dx in ORDER]
+    side = pix % 2
+    partners = [
+        ((y + dy + side * (dx - dy) + 4) % 4) * 4 + (x + dx + side * (dy - dx) + 4) % 4 for dy, dx in ORDER
+    ]
     lines = [(pix + d) % NPIX for d in range(1, NPIX)]
 
     barrier = pltpu.get_barrier_semaphore()

time: 107 us -> 106 us (level)
  no operation moved by 1% of the time
where the time goes in v4:
time: 106 us
  Pallas kernels  104 us (98%)
  local copies, waits for them, and re-layouts  2.02 us (2%)
    pallas_call x1, Pallas kernels, body(): pl.pallas_call(kernel, out_shape=pltpu.VMEM(prior_motion.shape, jnp.bfloa...  104 us

profile of v4, /device:TPU:1, one launch (start us, length us, event | category | flops | bytes accessed | tf_op | source)
XLA Modules:
  0.0 106.2 jit_solution(414287187178439454)
XLA Ops:
  0.0 104.1 %smoother.1 = bf16[4,16,32768]{2,1,0:T(8,128)(2,1)S(1)} custom-call(bf16[4,16,32768]{2,1,0:T(8,128)(2,1)} %prior.1, f32[1200]{0:T(1024)} %measured.1, f32[1200]{0:T(1024)} %stddev.1, f32[2,64,1200]{2,1,0:T(8,128)} %bitcast.1, s32[2,1200]{1,0:T(2,128)} %couples.1, s32[1200]{0:T(1024)} %tiles.1), custom_call_target="tpu_custom_call" | custom-call | tf_op jit(solution)/shard_map/smoother/pallas_call | solution.py:307
  104.1 2.0 %copy.8 = bf16[4,16,32768]{2,1,0:T(8,128)(2,1)} copy(bf16[4,16,32768]{2,1,0:T(8,128)(2,1)S(1)} %smoother.1) | data formatting | bytes 8388608
